TPU v7x, 32 devices: a whole 2x2x4 slice. The times are simulated.
32 devices in a mesh: seg: 16 (over z, y, x), slab: 2 (over core).
Axes of the slice: x: 2, y: 2, z: 4, core: 2. Of those that a mesh axis runs over, the one named last changes fastest.
Arguments:
- block: float32 [16, 4, 16, 4096], P('seg', None, 'slab'), may hold values from -6 to 6
- base_velocity: bfloat16 [16, 8, 2, 16, 4096], P('seg', None, None, 'slab'), may hold values from -6 to 6
Outputs:
- new_block: float32 [16, 4, 16, 4096], P('seg', None, 'slab')
All inputs are finite; a program needn't handle non-finite values.
Results may differ from a plain program's by a relative error of at most 0.0003.
Values may be sent and summed in bfloat16 or wider, within the bound.
No kernel may reach another device: no remote copies, remote signals or barrier semaphores. Data moves between devices by JAX's collectives and lax.ppermute only.
A program may use at most 64 MiB of HBM per device.

v0:
```python
import jax
import jax.numpy as jnp
from jax import lax
from jax.sharding import PartitionSpec as P

HOPS = 4


def with_halo(shard, sides, width):
    for axis, dim in sides:
        size, length = (lax.axis_size(axis), shard.shape[dim])
        up = [(i, (i + 1) % size) for i in range(size)]
        down = [(j, i) for i, j in up]
        last = lax.slice_in_dim(shard, length - width, length, axis=dim)
        first = lax.slice_in_dim(shard, 0, width, axis=dim)
        before = lax.ppermute(last, axis, up)
        after = lax.ppermute(first, axis, down)
        shard = jnp.concatenate([before, shard, after], axis=dim)
    return shard


def shifted(block, axis, distance):
    devices = range(lax.axis_size(axis))
    route = [((i - distance) % len(devices), i) for i in devices]
    return lax.ppermute(block, axis, route)


def advance(padded, velocity):
    centre = padded[:, 1:-1]
    up = padded[:, 2:]
    down = padded[:, :-2]
    east = jnp.roll(centre, -1, 2)
    west = jnp.roll(centre, 1, 2)
    speed_x = velocity[0].astype(jnp.float32)
    speed_y = velocity[1].astype(jnp.float32)
    return (
        centre
        + 0.2 * (up + down + east + west - 4.0 * centre)
        - 0.05 * (speed_x * (east - west) + speed_y * (up - down))
        - 0.02 * centre
    )


def lower_inverse(lower):
    count = lower.shape[0]
    rows = []
    for i in range(count):
        entries = []
        for j in range(count):
            if j > i:
                entries.append(jnp.zeros((), jnp.float32))
            elif j == i:
                entries.append(1.0 / lower[i, i])
            else:
                total = jnp.zeros((), jnp.float32)
                for k in range(j, i):
                    total = total + lower[i, k] * rows[k][j]
                entries.append(-total / lower[i, i])
        rows.append(entries)
    return jnp.stack([jnp.stack(r) for r in rows])


def shards(block, base_velocity):
    vectors = block[0]
    velocity = base_velocity[0]
    depth = velocity.shape[0]
    velocity_wide = with_halo(velocity, (("slab", 2),), depth)
    for hop in range(HOPS):
        moved = with_halo(vectors, (("slab", 1),), depth)
        for j in range(depth):
            height = velocity_wide.shape[2]
            moved = advance(moved, velocity_wide[j][:, j + 1 : height - j - 1])
        arrived = shifted(moved, "seg", 1)
        residual = arrived - vectors
        local_gram = jnp.einsum("ayx,byx->ab", residual, residual, precision=lax.Precision.HIGHEST)
        gram = lax.psum(local_gram, ("seg", "slab"))
        inverse = lower_inverse(jnp.linalg.cholesky(gram))
        vectors = jnp.einsum("ab,byx->ayx", inverse, residual, precision=lax.Precision.HIGHEST)
    return vectors[None]


def solution(mesh):
    placed = (P("seg", None, "slab", None), P("seg", None, None, "slab", None))
    return jax.shard_map(
        shards, mesh=mesh, in_specs=placed, out_specs=P("seg", None, "slab", None), check_vma=False
    )
```

profile of v0, /device:TPU:0, one launch (start us, length us, event | category | flops | bytes accessed | tf_op | source)
XLA Modules:
  0.0 402.6 jit_solution(13128962922173816920)
XLA Ops:
  0.0 1.4 copy.26
  5.7 1.5 collective-permute-done.2
  8.0 3.8 multiply_subtract_fusion.3
  12.8 2.1 multiply_subtract_fusion.7
  15.8 1.9 multiply_subtract_fusion.11
  18.5 1.6 multiply_subtract_fusion.15
  20.9 1.5 multiply_subtract_fusion.19
  23.0 1.1 multiply_subtract_fusion.23
  26.7 3.5 collective-permute-start.4
  30.2 16.2 %collective-permute-done.4 = f32[4,8,4096]{2,0,1:T(4,128)S(1)} collective-permute-done((f32[4,8,4096]{2,0,1:T(4,128)S(1)}, f32[4,8,4096]{2,0,1:T(4,128)S(1)}, u32[]{:S(2)}, u32[]{:S(2)}) %collective-permute-start.4) | collective-permute-done | bytes 524320 | tf_op jit(solution)/shard_map/ppermute | solution.py:25
  47.2 2.3 convolution_bitcast_fusion.4
  49.6 37.5 %psum.28 = f32[4,4]{0,1:T(4,128)S(1)} all-reduce(f32[4,4]{0,1:T(4,128)S(1)} %convolution_bitcast_fusion.4), channel_id=1, replica_groups=mesh['seg'=16,'slab'=2] {'seg','slab'}, use_global_device_ids=true, to_apply=%region_0.1 | all-reduce | flops 16 | bytes 128 | tf_op jit(solution)/shard_map/psum | solution.py:76
  102.4 2.5 fusion.24
  105.4 1.4 collective-permute-done.6
  109.0 3.5 multiply_subtract_fusion.2
  113.5 2.1 multiply_subtract_fusion.6
  116.3 1.9 multiply_subtract_fusion.10
  119.3 1.6 multiply_subtract_fusion.14
  121.6 1.7 multiply_subtract_fusion.18
  123.9 1.0 multiply_subtract_fusion.22
  128.5 2.3 collective-permute-start.7
  130.8 15.3 %collective-permute-done.7 = f32[4,8,4096]{2,0,1:T(4,128)S(1)} collective-permute-done((f32[4,8,4096]{2,0,1:T(4,128)S(1)}, f32[4,8,4096]{2,0,1:T(4,128)S(1)}, u32[]{:S(2)}, u32[]{:S(2)}) %collective-permute-start.7) | collective-permute-done | bytes 524320 | tf_op jit(solution)/shard_map/ppermute | solution.py:25
  146.2 2.3 convolution_bitcast_fusion.3
  148.6 38.1 %psum.29 = f32[4,4]{0,1:T(4,128)S(1)} all-reduce(f32[4,4]{0,1:T(4,128)S(1)} %convolution_bitcast_fusion.3), channel_id=1, replica_groups=mesh['seg'=16,'slab'=2] {'seg','slab'}, use_global_device_ids=true, to_apply=%region_3.5 | all-reduce | flops 16 | bytes 128 | tf_op jit(solution)/shard_map/psum | solution.py:76
  202.7 1.0 fusion.31
  204.3 1.4 collective-permute-done.9
  207.9 3.5 multiply_subtract_fusion.1
  212.3 2.1 multiply_subtract_fusion.5
  215.2 1.9 multiply_subtract_fusion.9
  218.2 1.6 multiply_subtract_fusion.13
  220.5 1.9 multiply_subtract_fusion.17
  223.5 1.1 multiply_subtract_fusion.21
  228.1 2.3 collective-permute-start.10
  230.5 15.3 %collective-permute-done.10 = f32[4,8,4096]{2,0,1:T(4,128)S(1)} collective-permute-done((f32[4,8,4096]{2,0,1:T(4,128)S(1)}, f32[4,8,4096]{2,0,1:T(4,128)S(1)}, u32[]{:S(2)}, u32[]{:S(2)}) %collective-permute-start.10) | collective-permute-done | bytes 524320 | tf_op jit(solution)/shard_map/ppermute | solution.py:25
  245.9 2.3 convolution_bitcast_fusion.2
  248.2 37.4 %psum.30 = f32[4,4]{0,1:T(4,128)S(1)} all-reduce(f32[4,4]{0,1:T(4,128)S(1)} %convolution_bitcast_fusion.2), channel_id=1, replica_groups=mesh['seg'=16,'slab'=2] {'seg','slab'}, use_global_device_ids=true, to_apply=%region_4.6 | all-reduce | flops 16 | bytes 128 | tf_op jit(solution)/shard_map/psum | solution.py:76
  303.2 1.4 collective-permute-done.12
  306.8 3.5 multiply_subtract_fusion
  311.3 2.1 multiply_subtract_fusion.4
  314.1 1.9 multiply_subtract_fusion.8
  317.1 1.6 multiply_subtract_fusion.12
  319.4 1.6 multiply_subtract_fusion.16
  322.2 1.0 multiply_subtract_fusion.20
  326.8 2.3 collective-permute-start.13
  329.1 15.3 %collective-permute-done.13 = f32[4,8,4096]{2,0,1:T(4,128)S(1)} collective-permute-done((f32[4,8,4096]{2,0,1:T(4,128)S(1)}, f32[4,8,4096]{2,0,1:T(4,128)S(1)}, u32[]{:S(2)}, u32[]{:S(2)}) %collective-permute-start.13) | collective-permute-done | bytes 524320 | tf_op jit(solution)/shard_map/ppermute | solution.py:25
  344.6 2.3 convolution_bitcast_fusion.1
  346.9 38.2 %psum.31 = f32[4,4]{0,1:T(4,128)S(1)} all-reduce(f32[4,4]{0,1:T(4,128)S(1)} %convolution_bitcast_fusion.1), channel_id=1, replica_groups=mesh['seg'=16,'slab'=2] {'seg','slab'}, use_global_device_ids=true, to_apply=%region_5.7 | all-reduce | flops 16 | bytes 128 | tf_op jit(solution)/shard_map/psum | solution.py:76
  401.3 1.1 copy.12
  (201 shorter events, 57.7 us)
Async XLA Ops:
  1.4 2.1 collective-permute-start.1
  1.9 2.3 collective-permute-start
  2.0 3.7 collective-permute-start.3
  2.5 4.8 %collective-permute-start.2 = (bf16[8,2,8,4096]{3,2,1,0:T(8,128)(2,1)}, bf16[8,2,8,4096]{3,2,1,0:T(8,128)(2,1)S(1)}, u32[]{:S(2)}, u32[]{:S(2)}) collective-permute-start(bf16[8,2,8,4096]{3,2,1,0:T(8,128)(2,1)} %bitcast.228), channel_id=1, source_target_pairs={{0,1},{1,0},{2,3},{3,2},{4,5},{5,4},{6,7},{7,6},{8,9},{9,8},{10,11... | collective-permute-start | bytes 3145736 | tf_op jit(solution)/shard_map/ppermute | solution.py:16
  4.8 2.4 copy-start.28
  18.5 1.6 copy-start.14
  18.5 1.6 copy-start.18
  23.0 100.8 %copy-start = (f32[12,4096]{1,0:T(8,128)}, f32[12,4096]{1,0:T(8,128)S(1)}, u32[]{:S(2)}) copy-start(f32[12,4096]{1,0:T(8,128)S(1)} %get-tuple-element.138) | copy-start | bytes 589828
  23.0 100.8 %copy-start.3 = (f32[12,4096]{1,0:T(8,128)}, f32[12,4096]{1,0:T(8,128)S(1)}, u32[]{:S(2)}) copy-start(f32[12,4096]{1,0:T(8,128)S(1)} %get-tuple-element.139) | copy-start | bytes 589828
  24.6 0.9 copy-start.6
  24.7 0.9 copy-start.10
  26.0 0.7 copy-start.23
  26.0 21.2 %copy-start.22 = (f32[1,4,8,4096]{3,2,1,0:T(8,128)S(1)}, f32[1,4,8,4096]{3,2,1,0:T(8,128)}, u32[]{:S(2)}) copy-start(f32[1,4,8,4096]{3,2,1,0:T(8,128)} %param.3) | copy-start | bytes 1572868
  26.7 19.7 %collective-permute-start.4 = (f32[4,8,4096]{2,0,1:T(4,128)S(1)}, f32[4,8,4096]{2,0,1:T(4,128)S(1)}, u32[]{:S(2)}, u32[]{:S(2)}) collective-permute-start(f32[4,8,4096]{2,0,1:T(4,128)S(1)} %multiply_subtract_fusion.31), channel_id=1, source_target_pairs={{30,0},{0,2},{2,4},{4,6},{6,8},{8,10},{10,12},{12,14},{14,16},{16,... | collective-permute-start | bytes 1572872 | tf_op jit(solution)/shard_map/ppermute | solution.py:25
  46.4 0.8 copy-start.27
  104.8 2.0 collective-permute-start.6
  104.9 2.6 collective-permute-start.5
  118.3 1.0 copy-start.15
  118.3 1.0 copy-start.19
  125.0 1.0 copy-start.7
  125.0 1.0 copy-start.11
  126.9 0.9 copy-start.24
  128.5 17.6 %collective-permute-start.7 = (f32[4,8,4096]{2,0,1:T(4,128)S(1)}, f32[4,8,4096]{2,0,1:T(4,128)S(1)}, u32[]{:S(2)}, u32[]{:S(2)}) collective-permute-start(f32[4,8,4096]{2,0,1:T(4,128)S(1)} %multiply_subtract_fusion.30), channel_id=1, source_target_pairs={{30,0},{0,2},{2,4},{4,6},{6,8},{8,10},{10,12},{12,14},{14,16},{16,... | collective-permute-start | bytes 1572872 | tf_op jit(solution)/shard_map/ppermute | solution.py:25
  203.7 2.0 collective-permute-start.9
  203.8 2.6 collective-permute-start.8
  217.2 1.0 copy-start.16
  217.2 1.0 copy-start.20
  222.5 1.0 copy-start.1
  222.5 1.0 copy-start.4
  224.6 1.0 copy-start.8
  224.6 1.0 copy-start.12
  226.5 0.9 copy-start.25
  228.1 17.6 %collective-permute-start.10 = (f32[4,8,4096]{2,0,1:T(4,128)S(1)}, f32[4,8,4096]{2,0,1:T(4,128)S(1)}, u32[]{:S(2)}, u32[]{:S(2)}) collective-permute-start(f32[4,8,4096]{2,0,1:T(4,128)S(1)} %multiply_subtract_fusion.29), channel_id=1, source_target_pairs={{30,0},{0,2},{2,4},{4,6},{6,8},{8,10},{10,12},{12,14},{14,16},{16,... | collective-permute-start | bytes 1572872 | tf_op jit(solution)/shard_map/ppermute | solution.py:25
  302.6 2.0 collective-permute-start.12
  302.7 2.6 collective-permute-start.11
  316.1 1.0 copy-start.17
  316.1 1.0 copy-start.21
  321.1 1.0 copy-start.2
  321.1 1.0 copy-start.5
  323.3 1.0 copy-start.9
  323.3 1.0 copy-start.13
  325.2 0.9 copy-start.26
  326.8 17.6 %collective-permute-start.13 = (f32[4,8,4096]{2,0,1:T(4,128)S(1)}, f32[4,8,4096]{2,0,1:T(4,128)S(1)}, u32[]{:S(2)}, u32[]{:S(2)}) collective-permute-start(f32[4,8,4096]{2,0,1:T(4,128)S(1)} %multiply_subtract_fusion.28), channel_id=1, source_target_pairs={{30,0},{0,2},{2,4},{4,6},{6,8},{8,10},{10,12},{12,14},{14,16},{16,... | collective-permute-start | bytes 1572872 | tf_op jit(solution)/shard_map/ppermute | solution.py:25
where the time goes:
time: 407 us; the launch traced here: 403 us
  blocking collectives  151 us (37%)
  waiting for transfers between devices  71.7 us (18%)
  other arithmetic  65.1 us (16%)
  between operations  52.8 us (13%)
  local copies, waits for them, and re-layouts  33.8 us (8%)
  matrix products  14.7 us (4%)
  starting transfers between devices  13.3 us (3%)
    psum x4, blocking collectives, shards(): gram = lax.psum(local_gram, ('seg', 'slab'))  151 us
    ppermute x4, waiting for transfers between devices, shifted(): return lax.ppermute(block, axis, route)  62.1 us
    sub x32, other arithmetic, advance(): centre + 0.2 * (up + down + east + west - 4.0 * centre)  53.8 us
    slice x60, local copies, waits for them, and re-layouts, advance(): east = jnp.roll(centre, -1, 2)  21.5 us
    ppermute x4, starting transfers between devices, shifted(): return lax.ppermute(block, axis, route)  10.5 us
    dot_general x4, matrix products, shards(): jnp.einsum('ayx,byx->ab', residual, residual, precision=lax.Precision.HIG...  9.32 us
  transfers between devices with their start and end apart: 14, of which 13 were waited for; matrix products, arithmetic and copies ran while one was open for 0% of the time, Pallas kernels for 0%

commit v1 on v0

--- a/solution.py
+++ b/solution.py
@@ -73,7 +73,9 @@
         arrived = shifted(moved, "seg", 1)
         residual = arrived - vectors
         local_gram = jnp.einsum("ayx,byx->ab", residual, residual, precision=lax.Precision.HIGHEST)
-        gram = lax.psum(local_gram, ("seg", "slab"))
+        gram = local_gram
+        for name in ("slab", "seg"):
+            gram = lax.psum(gram, name)
         inverse = lower_inverse(jnp.linalg.cholesky(gram))
         vectors = jnp.einsum("ab,byx->ayx", inverse, residual, precision=lax.Precision.HIGHEST)
     return vectors[None]

time: 407 us -> 411 us (level)
  blocking collectives: 151 us -> 158 us
    psum x4 -> x8, blocking collectives: 151 us -> 158 us  [shards(): gram = lax.psum(gram, name)]
where the time goes in v1:
time: 411 us; the launch traced here: 408 us
  blocking collectives  158 us (38%)
  waiting for transfers between devices  74.3 us (18%)
  other arithmetic  64.9 us (16%)
  between operations  51.5 us (13%)
  local copies, waits for them, and re-layouts  33.8 us (8%)
  matrix products  14.7 us (4%)
  starting transfers between devices  10.8 us (3%)
    psum x8, blocking collectives, shards(): gram = lax.psum(gram, name)  158 us
    ppermute x4, waiting for transfers between devices, shifted(): return lax.ppermute(block, axis, route)  64.6 us
    sub x32, other arithmetic, advance(): centre + 0.2 * (up + down + east + west - 4.0 * centre)  53.8 us
    slice x60, local copies, waits for them, and re-layouts, advance(): east = jnp.roll(centre, -1, 2)  21.5 us
    dot_general x4, matrix products, shards(): jnp.einsum('ayx,byx->ab', residual, residual, precision=lax.Precision.HIG...  9.32 us
  transfers between devices with their start and end apart: 14, of which 13 were waited for; matrix products, arithmetic and copies ran while one was open for 0% of the time, Pallas kernels for 0%

profile of v1, /device:TPU:0, one launch (start us, length us, event | category | flops | bytes accessed | tf_op | source)
XLA Modules:
  0.0 407.7 jit_solution(3839665061770412189)
XLA Ops:
  0.0 1.4 copy.26
  5.7 1.5 collective-permute-done.2
  8.0 3.8 multiply_subtract_fusion.3
  12.8 2.1 multiply_subtract_fusion.7
  15.8 1.9 multiply_subtract_fusion.11
  18.5 1.6 multiply_subtract_fusion.15
  20.9 1.5 multiply_subtract_fusion.19
  23.0 1.1 multiply_subtract_fusion.23
  26.7 3.5 collective-permute-start.4
  30.2 16.2 %collective-permute-done.4 = f32[4,8,4096]{2,0,1:T(4,128)S(1)} collective-permute-done((f32[4,8,4096]{2,0,1:T(4,128)S(1)}, f32[4,8,4096]{2,0,1:T(4,128)S(1)}, u32[]{:S(2)}, u32[]{:S(2)}) %collective-permute-start.4) | collective-permute-done | bytes 524320 | tf_op jit(solution)/shard_map/ppermute | solution.py:25
  47.2 2.3 convolution_bitcast_fusion.4
  49.6 2.5 psum.56
  52.0 38.3 %psum.57 = f32[4,4]{0,1:T(4,128)S(1)} all-reduce(f32[4,4]{0,1:T(4,128)S(1)} %psum.56), channel_id=1, replica_groups=mesh['seg'=16,'slab'=2] {'seg'}, use_global_device_ids=true, to_apply=%region_1.2 | all-reduce | flops 16 | bytes 128 | tf_op jit(solution)/shard_map/psum | solution.py:78
  105.4 2.5 fusion.24
  108.4 1.4 collective-permute-done.6
  112.0 3.5 multiply_subtract_fusion.2
  116.5 2.1 multiply_subtract_fusion.6
  119.3 1.9 multiply_subtract_fusion.10
  122.3 1.6 multiply_subtract_fusion.14
  124.6 1.7 multiply_subtract_fusion.18
  131.8 17.3 %collective-permute-done.7 = f32[4,8,4096]{2,0,1:T(4,128)S(1)} collective-permute-done((f32[4,8,4096]{2,0,1:T(4,128)S(1)}, f32[4,8,4096]{2,0,1:T(4,128)S(1)}, u32[]{:S(2)}, u32[]{:S(2)}) %collective-permute-start.7) | collective-permute-done | bytes 524320 | tf_op jit(solution)/shard_map/ppermute | solution.py:25
  149.2 2.3 convolution_bitcast_fusion.3
  151.6 2.5 psum.58
  154.0 36.5 %psum.59 = f32[4,4]{0,1:T(4,128)S(1)} all-reduce(f32[4,4]{0,1:T(4,128)S(1)} %psum.58), channel_id=1, replica_groups=mesh['seg'=16,'slab'=2] {'seg'}, use_global_device_ids=true, to_apply=%region_5.7 | all-reduce | flops 16 | bytes 128 | tf_op jit(solution)/shard_map/psum | solution.py:78
  207.3 1.4 collective-permute-done.9
  211.0 3.5 multiply_subtract_fusion.1
  215.4 2.1 multiply_subtract_fusion.5
  218.3 1.9 multiply_subtract_fusion.9
  221.3 1.6 multiply_subtract_fusion.13
  223.5 1.9 multiply_subtract_fusion.17
  226.5 1.1 multiply_subtract_fusion.21
  231.2 2.1 collective-permute-start.10
  233.3 15.6 %collective-permute-done.10 = f32[4,8,4096]{2,0,1:T(4,128)S(1)} collective-permute-done((f32[4,8,4096]{2,0,1:T(4,128)S(1)}, f32[4,8,4096]{2,0,1:T(4,128)S(1)}, u32[]{:S(2)}, u32[]{:S(2)}) %collective-permute-start.10) | collective-permute-done | bytes 524320 | tf_op jit(solution)/shard_map/ppermute | solution.py:25
  248.9 2.3 convolution_bitcast_fusion.2
  251.3 2.5 psum.60
  253.7 36.5 %psum.61 = f32[4,4]{0,1:T(4,128)S(1)} all-reduce(f32[4,4]{0,1:T(4,128)S(1)} %psum.60), channel_id=1, replica_groups=mesh['seg'=16,'slab'=2] {'seg'}, use_global_device_ids=true, to_apply=%region_7.9 | all-reduce | flops 16 | bytes 128 | tf_op jit(solution)/shard_map/psum | solution.py:78
  307.0 1.4 collective-permute-done.12
  310.7 3.5 multiply_subtract_fusion
  315.1 2.1 multiply_subtract_fusion.4
  318.0 1.9 multiply_subtract_fusion.8
  321.0 1.6 multiply_subtract_fusion.12
  323.2 1.6 multiply_subtract_fusion.16
  330.6 2.1 collective-permute-start.13
  332.7 15.6 %collective-permute-done.13 = f32[4,8,4096]{2,0,1:T(4,128)S(1)} collective-permute-done((f32[4,8,4096]{2,0,1:T(4,128)S(1)}, f32[4,8,4096]{2,0,1:T(4,128)S(1)}, u32[]{:S(2)}, u32[]{:S(2)}) %collective-permute-start.13) | collective-permute-done | bytes 524320 | tf_op jit(solution)/shard_map/ppermute | solution.py:25
  348.4 2.3 convolution_bitcast_fusion.1
  350.7 2.5 psum.62
  353.2 36.5 %psum.63 = f32[4,4]{0,1:T(4,128)S(1)} all-reduce(f32[4,4]{0,1:T(4,128)S(1)} %psum.62), channel_id=1, replica_groups=mesh['seg'=16,'slab'=2] {'seg'}, use_global_device_ids=true, to_apply=%region_9.11 | all-reduce | flops 16 | bytes 128 | tf_op jit(solution)/shard_map/psum | solution.py:78
  406.4 1.1 copy.12
  (205 shorter events, 60.9 us)
Async XLA Ops:
  1.4 2.1 collective-permute-start.1
  1.9 2.3 collective-permute-start
  2.0 3.7 collective-permute-start.3
  2.5 4.8 %collective-permute-start.2 = (bf16[8,2,8,4096]{3,2,1,0:T(8,128)(2,1)}, bf16[8,2,8,4096]{3,2,1,0:T(8,128)(2,1)S(1)}, u32[]{:S(2)}, u32[]{:S(2)}) collective-permute-start(bf16[8,2,8,4096]{3,2,1,0:T(8,128)(2,1)} %bitcast.228), channel_id=1, source_target_pairs={{0,1},{1,0},{2,3},{3,2},{4,5},{5,4},{6,7},{7,6},{8,9},{9,8},{10,11... | collective-permute-start | bytes 3145736 | tf_op jit(solution)/shard_map/ppermute | solution.py:16
  4.8 2.4 copy-start.28
  18.5 1.6 copy-start.14
  18.5 1.6 copy-start.18
  23.0 103.8 %copy-start = (f32[12,4096]{1,0:T(8,128)}, f32[12,4096]{1,0:T(8,128)S(1)}, u32[]{:S(2)}) copy-start(f32[12,4096]{1,0:T(8,128)S(1)} %get-tuple-element.138) | copy-start | bytes 589828
  23.0 103.8 %copy-start.3 = (f32[12,4096]{1,0:T(8,128)}, f32[12,4096]{1,0:T(8,128)S(1)}, u32[]{:S(2)}) copy-start(f32[12,4096]{1,0:T(8,128)S(1)} %get-tuple-element.139) | copy-start | bytes 589828
  24.6 0.9 copy-start.6
  24.7 0.9 copy-start.10
  26.0 0.7 copy-start.23
  26.0 21.2 %copy-start.22 = (f32[1,4,8,4096]{3,2,1,0:T(8,128)S(1)}, f32[1,4,8,4096]{3,2,1,0:T(8,128)}, u32[]{:S(2)}) copy-start(f32[1,4,8,4096]{3,2,1,0:T(8,128)} %param.3) | copy-start | bytes 1572868
  26.7 19.7 %collective-permute-start.4 = (f32[4,8,4096]{2,0,1:T(4,128)S(1)}, f32[4,8,4096]{2,0,1:T(4,128)S(1)}, u32[]{:S(2)}, u32[]{:S(2)}) collective-permute-start(f32[4,8,4096]{2,0,1:T(4,128)S(1)} %multiply_subtract_fusion.31), channel_id=1, source_target_pairs={{30,0},{0,2},{2,4},{4,6},{6,8},{8,10},{10,12},{12,14},{14,16},{16,... | collective-permute-start | bytes 1572872 | tf_op jit(solution)/shard_map/ppermute | solution.py:25
  46.4 0.8 copy-start.27
  107.8 2.0 collective-permute-start.6
  107.9 2.6 collective-permute-start.5
  121.3 1.0 copy-start.15
  121.3 1.0 copy-start.19
  128.0 1.0 copy-start.7
  128.0 1.0 copy-start.11
  129.9 0.9 copy-start.24
  131.5 17.6 %collective-permute-start.7 = (f32[4,8,4096]{2,0,1:T(4,128)S(1)}, f32[4,8,4096]{2,0,1:T(4,128)S(1)}, u32[]{:S(2)}, u32[]{:S(2)}) collective-permute-start(f32[4,8,4096]{2,0,1:T(4,128)S(1)} %multiply_subtract_fusion.30), channel_id=1, source_target_pairs={{30,0},{0,2},{2,4},{4,6},{6,8},{8,10},{10,12},{12,14},{14,16},{16,... | collective-permute-start | bytes 1572872 | tf_op jit(solution)/shard_map/ppermute | solution.py:25
  206.8 2.0 collective-permute-start.9
  206.8 2.6 collective-permute-start.8
  220.2 1.0 copy-start.16
  220.2 1.0 copy-start.20
  225.5 1.0 copy-start.1
  225.5 1.0 copy-start.4
  227.7 1.0 copy-start.8
  227.7 1.0 copy-start.12
  229.6 0.9 copy-start.25
  231.2 17.6 %collective-permute-start.10 = (f32[4,8,4096]{2,0,1:T(4,128)S(1)}, f32[4,8,4096]{2,0,1:T(4,128)S(1)}, u32[]{:S(2)}, u32[]{:S(2)}) collective-permute-start(f32[4,8,4096]{2,0,1:T(4,128)S(1)} %multiply_subtract_fusion.29), channel_id=1, source_target_pairs={{30,0},{0,2},{2,4},{4,6},{6,8},{8,10},{10,12},{12,14},{14,16},{16,... | collective-permute-start | bytes 1572872 | tf_op jit(solution)/shard_map/ppermute | solution.py:25
  306.5 2.0 collective-permute-start.12
  306.5 2.6 collective-permute-start.11
  319.9 1.0 copy-start.17
  319.9 1.0 copy-start.21
  325.0 1.0 copy-start.2
  325.0 1.0 copy-start.5
  327.1 1.0 copy-start.9
  327.1 1.0 copy-start.13
  329.0 0.9 copy-start.26
  330.6 17.6 %collective-permute-start.13 = (f32[4,8,4096]{2,0,1:T(4,128)S(1)}, f32[4,8,4096]{2,0,1:T(4,128)S(1)}, u32[]{:S(2)}, u32[]{:S(2)}) collective-permute-start(f32[4,8,4096]{2,0,1:T(4,128)S(1)} %multiply_subtract_fusion.28), channel_id=1, source_target_pairs={{30,0},{0,2},{2,4},{4,6},{6,8},{8,10},{10,12},{12,14},{14,16},{16,... | collective-permute-start | bytes 1572872 | tf_op jit(solution)/shard_map/ppermute | solution.py:25
